TPU v7x, 256 devices: a whole 4x4x8 slice. The times are simulated.
256 devices in a mesh: dp: 2 (over core), section: 8 (over z), mp: 16 (over y, x).
Axes of the slice: x: 4, y: 4, z: 8, core: 2. Of those that a mesh axis runs over, the one named last changes fastest.
Arguments:
- inputs: bfloat16 [192, 512], P(('dp', 'mp')), may hold values from -6 to 6
- tangents: bfloat16 [192, 32, 512], P(('dp', 'mp')), may hold values from -6 to 6
- targets: bfloat16 [192, 1024], P(('dp', 'mp')), may hold values from -24 to 24
- target_jac: bfloat16 [192, 32, 1024], P(('dp', 'mp')), may hold values from -24 to 24
- rank_mask: int32 [192, 32], P(('dp', 'mp')), may hold values from 0 to 1, as said below
- batch_order: int32 [32, 6], P(('dp', 'mp')), may hold values from 0 to 5, each once within a row
- encoder: bfloat16 [512, 2048], replicated, may hold values from -0.25 to 0.25
- layers: bfloat16 [8, 2048, 2048], P('section', 'mp'), may hold values from -0.125 to 0.125
- head_weight: bfloat16 [2048, 1024], replicated, may hold values from -0.125 to 0.125
Outputs:
- grad_layers: float32 [8, 2048, 2048], P('section', ('dp', 'mp'))
- grad_head: float32 [2048, 1024], P(('dp', 'mp'), 'section')
- loss_value: float32 [], replicated
Inputs may be any that keep to these rules, and one draw needn't show every extreme that they name: `rank_mask`: each sample's ones are its first 1 to 32 directions. `batch_order`: each row is an ordering of 0 .. 5.
All inputs are finite; a program needn't handle non-finite values.
Results may differ from a plain program's by a relative error of at most 0.035.
Values may be sent and summed in bfloat16 or wider, within the bound.
A program may use at most 128 MiB of HBM per device.

v0:
```python
import jax
import jax.numpy as jnp
from jax import lax
from jax.sharding import PartitionSpec as P

MB = 6


def from_behind(value, axis, steps):
    count = lax.axis_size(axis)
    initial, last = (max(0, -steps), min(count, count - steps))
    return lax.ppermute(value, axis, [(source, source + steps) for source in range(initial, last)])


def in_blocks(array, dim, count):
    before, after = (array.shape[:dim], array.shape[dim + 1 :])
    return jnp.moveaxis(array.reshape(*before, count, -1, *after), dim, 0)


def sent_and_summed(array, axis, dim):
    parts = in_blocks(array, dim, lax.axis_size(axis))
    arrived = lax.all_to_all(parts, axis, split_axis=0, concat_axis=0, tiled=True)
    return arrived.astype(jnp.float32).sum(axis=0)


def from_everyone(array, axis):
    count = lax.axis_size(axis)
    return lax.all_to_all(
        jnp.broadcast_to(array[None], (count, *array.shape)), axis, 0, 0, tiled=True
    )


def over_copies(array, axis):
    return from_everyone(array, axis).sum(axis=0)


def forward_layer(row_block, weight):
    model_width = weight.shape[1]
    pre_act = jnp.dot(
        row_block.reshape(-1, model_width), weight, preferred_element_type=jnp.float32
    ).reshape(row_block.shape)
    tanh_p = jnp.tanh(pre_act[:, 0])
    slope_vals = 1.0 - tanh_p * tanh_p
    primal = row_block[:, 0].astype(jnp.float32) + tanh_p
    tangent = row_block[:, 1:].astype(jnp.float32) + slope_vals[:, None, :] * pre_act[:, 1:]
    return (jnp.concatenate([primal[:, None], tangent], axis=1).astype(jnp.bfloat16), pre_act)


def backward_layer(pre_act, grad_rows, weight):
    model_width = weight.shape[1]
    upstream = grad_rows.astype(jnp.float32)
    tanh_p = jnp.tanh(pre_act[:, 0])
    slope_vals = 1.0 - tanh_p * tanh_p
    tangent_part = upstream[:, 1:] * slope_vals[:, None, :]
    slope_grad = jnp.sum(upstream[:, 1:] * pre_act[:, 1:], axis=1)
    primal_part = upstream[:, 0] * slope_vals - 2.0 * slope_grad * tanh_p * slope_vals
    grad_mix = jnp.concatenate([primal_part[:, None], tangent_part], axis=1).astype(jnp.bfloat16)
    back_rows = jnp.dot(
        grad_mix.reshape(-1, model_width), weight.T, preferred_element_type=jnp.float32
    ).reshape(upstream.shape)
    return (grad_mix, (upstream + back_rows).astype(jnp.bfloat16))


def place_slot(store, value, batch_slot, is_valid):
    return lax.dynamic_update_index_in_dim(
        store, jnp.where(is_valid, value, store[batch_slot]), batch_slot, 0
    )


def local(
    inputs, tangents, targets, target_jac, rank_mask, batch_order, encoder, layers, head_weight
):
    samp_dev = inputs.shape[0]
    per_batch = samp_dev // MB
    row_depth = tangents.shape[1] + 1
    in_width = inputs.shape[1]
    model_width = layers.shape[2]
    out_width = head_weight.shape[1]
    sections = lax.axis_size("section")
    section_id = lax.axis_index("section")
    is_first = section_id == 0
    is_last = section_id == sections - 1
    layer_full = lax.all_gather(layers[0], "mp", axis=0, tiled=True)
    sample_order = batch_order[0]
    row_weight = jnp.concatenate(
        [jnp.ones((samp_dev, 1), jnp.float32), rank_mask.astype(jnp.float32)], axis=1
    )
    sample_total = jnp.sum(row_weight, axis=1)
    batch_counts = lax.psum(
        jnp.sum(sample_total[sample_order].reshape(MB, per_batch), axis=1), "mp"
    )

    def picked_of(batch_slot):
        return lax.dynamic_slice_in_dim(sample_order, batch_slot * per_batch, per_batch)

    def lift_batch(batch_slot):
        picked = picked_of(batch_slot)
        rows_in = jnp.concatenate([inputs[picked][:, None, :], tangents[picked]], axis=1)
        lifted = jnp.dot(rows_in.reshape(-1, in_width), encoder, preferred_element_type=jnp.float32)
        return lifted.reshape(per_batch, row_depth, model_width).astype(jnp.bfloat16)

    block_shape = (MB, per_batch, row_depth, model_width)
    pre_shape = (1, 1, 1, 1)

    def forward_tick(step_index, loop_state):
        incoming, store_in, store_pre, store_out = loop_state
        batch_index = step_index - section_id
        is_valid = (batch_index >= 0) & (batch_index < MB)
        batch_slot = jnp.clip(batch_index, 0, MB - 1)
        row_block = lax.cond(is_first, lambda: lift_batch(batch_slot), lambda: incoming)

        def forward_active():
            return forward_layer(row_block, layer_full)

        def forward_resting():
            return (row_block, jnp.zeros(row_block.shape, jnp.float32))

        layer_out, pre_act = lax.cond(is_valid, forward_active, forward_resting)
        store_in = place_slot(store_in, row_block, batch_slot, is_valid)
        store_out = place_slot(store_out, layer_out, batch_slot, is_valid)
        passed = from_behind(layer_out, "section", 1)
        return (passed, store_in, store_pre, store_out)

    start_state = (
        jnp.zeros(block_shape[1:], jnp.bfloat16),
        jnp.zeros(block_shape, jnp.bfloat16),
        jnp.zeros(pre_shape, jnp.float32),
        jnp.zeros(block_shape, jnp.bfloat16),
    )
    _, store_in, store_pre, store_out = lax.fori_loop(
        0, MB + sections - 1, forward_tick, start_state
    )

    def backward_tick(step_index, loop_state):
        incoming, store_mix, store_head, loss_acc = loop_state
        batch_index = step_index - (sections - 1 - section_id)
        is_valid = (batch_index >= 0) & (batch_index < MB)
        batch_slot = jnp.clip(batch_index, 0, MB - 1)
        batch_total = batch_counts[batch_slot]

        def head_part():
            final_rows = store_out[batch_slot]
            outputs = jnp.dot(
                final_rows.reshape(-1, model_width), head_weight, preferred_element_type=jnp.float32
            )
            outputs = outputs.reshape(per_batch, row_depth, out_width)
            picked = picked_of(batch_slot)
            wanted = jnp.concatenate(
                [targets[picked][:, None, :], target_jac[picked]], axis=1
            ).astype(jnp.float32)
            weights_here = row_weight[picked]
            mismatch = outputs - wanted
            misfit = jnp.sum(weights_here[:, :, None] * mismatch * mismatch) / batch_total
            cot_out = (2.0 * weights_here[:, :, None] * mismatch / batch_total).astype(jnp.bfloat16)
            grad_rows = jnp.dot(
                cot_out.reshape(-1, out_width), head_weight.T, preferred_element_type=jnp.float32
            )
            return (
                grad_rows.reshape(per_batch, row_depth, model_width).astype(jnp.bfloat16),
                cot_out,
                misfit,
            )

        def pass_on():
            return (
                incoming,
                jnp.zeros((per_batch, row_depth, out_width), jnp.bfloat16),
                jnp.zeros((), jnp.float32),
            )

        grad_rows, cot_out, misfit = lax.cond(is_last & is_valid, head_part, pass_on)

        def backward_active():
            row_block = store_in[batch_slot]
            pre_act = jnp.dot(
                row_block.reshape(-1, model_width), layer_full, preferred_element_type=jnp.float32
            ).reshape(row_block.shape)
            return backward_layer(pre_act, grad_rows, layer_full)

        def backward_resting():
            return (jnp.zeros(grad_rows.shape, jnp.bfloat16), grad_rows)

        grad_mix, grad_in = lax.cond(is_valid, backward_active, backward_resting)
        store_mix = place_slot(store_mix, grad_mix, batch_slot, is_valid)
        store_head = place_slot(store_head, cot_out, batch_slot, is_valid)
        loss_acc = loss_acc + jnp.where(is_valid, misfit, jnp.zeros((), jnp.float32))
        passed = from_behind(grad_in, "section", -1)
        return (passed, store_mix, store_head, loss_acc)

    back_state = (
        jnp.zeros(block_shape[1:], jnp.bfloat16),
        jnp.zeros(block_shape, jnp.bfloat16),
        jnp.zeros((MB, per_batch, row_depth, out_width), jnp.bfloat16),
        jnp.zeros((), jnp.float32),
    )
    _, store_mix, store_head, loss_acc = lax.fori_loop(
        0, MB + sections - 1, backward_tick, back_state
    )
    shard_rows = model_width // (lax.axis_size("dp") * lax.axis_size("mp"))
    in_flat = store_in.reshape(-1, model_width)
    mix_flat = store_mix.reshape(-1, model_width)
    grad_layers = lax.psum_scatter(
        jnp.dot(in_flat.T, mix_flat, preferred_element_type=jnp.float32).astype(jnp.bfloat16),
        ("dp", "mp"),
        scatter_dimension=0,
        tiled=True,
    ).astype(jnp.float32)[None]
    out_flat = store_out.reshape(-1, model_width)
    head_flat = store_head.reshape(-1, out_width)

    def compute():
        return jnp.dot(out_flat.T, head_flat, preferred_element_type=jnp.float32)

    def skipped():
        return jnp.zeros((shard_rows * lax.axis_size(("dp", "mp")), out_width), jnp.float32)

    summed = sent_and_summed(
        lax.cond(is_last, compute, skipped).astype(jnp.bfloat16), ("dp", "mp"), 0
    )
    section_loss = over_copies(loss_acc, ("dp", "mp"))
    loss_row = jnp.broadcast_to(section_loss, (1, sections))
    grad_head, loss_cols = (
        sent_and_summed(summed.astype(jnp.bfloat16), "section", 1),
        sent_and_summed(loss_row.astype(jnp.bfloat16), "section", 1),
    )
    loss_value = loss_cols[0, 0] / (lax.axis_size("dp") * MB * out_width)
    return (grad_layers, grad_head, loss_value)


def solution(mesh):
    in_specs = (
        P(("dp", "mp"), None),
        P(("dp", "mp"), None, None),
        P(("dp", "mp"), None),
        P(("dp", "mp"), None, None),
        P(("dp", "mp"), None),
        P(("dp", "mp"), None),
        P(),
        P("section", "mp", None),
        P(),
    )
    out_specs = (P("section", ("dp", "mp"), None), P(("dp", "mp"), "section"), P())
    return jax.shard_map(local, mesh=mesh, in_specs=in_specs, out_specs=out_specs, check_vma=False)
```

profile of v0, /device:TPU:4, one launch (start us, length us, event | category | flops | bytes accessed | tf_op | source)
XLA Modules:
  0.0 672.2 jit_solution(17826597853342746980)
XLA Ops:
  10.1 36.6 %psum.7 = f32[6]{0:T(128)S(1)} all-reduce(f32[6]{0:T(128)S(1)} %gather_fusion), channel_id=1, replica_groups=mesh['dp'=2,'section'=8,'mp'=16] {'mp'}, use_global_device_ids=true, to_apply=%region_7.0 | all-reduce | flops 6 | bytes 48 | tf_op jit(solution)/shard_map/psum | solution.py:89
  46.7 42.4 %all-gather.3.cloned.1.call-done = bf16[1,2048,2048]{2,1,0:T(8,128)(2,1)} async-done(((bf16[1,128,2048]{2,1,0:T(8,128)(2,1)}), bf16[1,2048,2048]{2,1,0:T(8,128)(2,1)}) %all-gather.3.cloned.1.call-update) | async-done | bytes 8388624 | tf_op jit(solution)/shard_map/all_gather | solution.py:83
  89.4 174.7 %while.49 = (s32[]{:T(128)}, bf16[1,33,2048]{2,1,0:T(8,128)(2,1)S(1)}, bf16[6,1,33,2048]{3,2,1,0:T(8,128)(2,1)S(1)}, bf16[6,1,33,2048]{3,2,1,0:T(8,128)(2,1)S(1)...) while((s32[]{:T(128)}, ...), condition=%wide.region_5.0_spmd, body=%wide.region_0.5_spmd.sunk | while | flops 346843136 | bytes 14290341 | solution.py:130
  89.5 6.7 conditional.10
  138.3 6.7 conditional.10
  170.3 6.7 conditional.10
  198.7 6.7 conditional.10
  265.3 276.2 %while.50 = (s32[]{:T(128)}, bf16[1,33,2048]{2,1,0:T(8,128)(2,1)S(1)}, bf16[6,1,33,2048]{3,2,1,0:T(8,128)(2,1)}, bf16[6,1,33,1024]{3,2,1,0:T(8,128)(2,1)S(1)}, f...) while((s32[]{:T(128)}, ...), condition=%wide.region_15.16_spmd, body=%wide.region_8.15_spmd.sunk | while | flops 832231424 | bytes 80654912 | solution.py:196
  317.9 73.0 %collective-permute-done.1 = bf16[1,33,2048]{2,1,0:T(8,128)(2,1)S(1)} collective-permute-done((bf16[1,33,2048]{2,1,0:T(8,128)(2,1)S(1)}, bf16[1,33,2048]{2,1,0:T(8,128)(2,1)S(1)}, u32[]{:S(2)}, u32[]{:S(2)}) %collective-permute-start.1) | collective-permute-done | bytes 135200 | tf_op jit(solution)/shard_map/while/body/eval_jaxpr/ppermute | solution.py:12
  391.6 8.5 %conditional.13 = (bf16[1,33,2048]{2,1,0:T(8,128)(2,1)S(1)}, bf16[1,33,2048]{2,1,0:T(8,128)(2,1)S(1)}) conditional(s32[]{:T(128)} %convert_element_type.144, bf16[1,33,2048]{2,1,0:T(8,128)(2,1)S(1)} %get-tuple-element.973, (bf16[1,33,2048]{2,1,0:T(8,128)(2,1)S(1)}, s32[]{:T(128)}, bf16[6,1,33,2048]{3,2,1,0:T(8,128)(2,1)S(1)}, ...), branch_computations={%region_12.12_spmd, %region_13.14_spmd} | conditional | flops 554866688 | bytes 53235792 | solution.py:183
  403.9 13.5 %collective-permute-done.1 = bf16[1,33,2048]{2,1,0:T(8,128)(2,1)S(1)} collective-permute-done((bf16[1,33,2048]{2,1,0:T(8,128)(2,1)S(1)}, bf16[1,33,2048]{2,1,0:T(8,128)(2,1)S(1)}, u32[]{:S(2)}, u32[]{:S(2)}) %collective-permute-start.1) | collective-permute-done | bytes 135200 | tf_op jit(solution)/shard_map/while/body/eval_jaxpr/ppermute | solution.py:12
  418.1 8.5 %conditional.13 = (bf16[1,33,2048]{2,1,0:T(8,128)(2,1)S(1)}, bf16[1,33,2048]{2,1,0:T(8,128)(2,1)S(1)}) conditional(s32[]{:T(128)} %convert_element_type.144, bf16[1,33,2048]{2,1,0:T(8,128)(2,1)S(1)} %get-tuple-element.973, (bf16[1,33,2048]{2,1,0:T(8,128)(2,1)S(1)}, s32[]{:T(128)}, bf16[6,1,33,2048]{3,2,1,0:T(8,128)(2,1)S(1)}, ...), branch_computations={%region_12.12_spmd, %region_13.14_spmd} | conditional | flops 554866688 | bytes 53235792 | solution.py:183
  430.5 13.6 %collective-permute-done.1 = bf16[1,33,2048]{2,1,0:T(8,128)(2,1)S(1)} collective-permute-done((bf16[1,33,2048]{2,1,0:T(8,128)(2,1)S(1)}, bf16[1,33,2048]{2,1,0:T(8,128)(2,1)S(1)}, u32[]{:S(2)}, u32[]{:S(2)}) %collective-permute-start.1) | collective-permute-done | bytes 135200 | tf_op jit(solution)/shard_map/while/body/eval_jaxpr/ppermute | solution.py:12
  444.7 8.5 %conditional.13 = (bf16[1,33,2048]{2,1,0:T(8,128)(2,1)S(1)}, bf16[1,33,2048]{2,1,0:T(8,128)(2,1)S(1)}) conditional(s32[]{:T(128)} %convert_element_type.144, bf16[1,33,2048]{2,1,0:T(8,128)(2,1)S(1)} %get-tuple-element.973, (bf16[1,33,2048]{2,1,0:T(8,128)(2,1)S(1)}, s32[]{:T(128)}, bf16[6,1,33,2048]{3,2,1,0:T(8,128)(2,1)S(1)}, ...), branch_computations={%region_12.12_spmd, %region_13.14_spmd} | conditional | flops 554866688 | bytes 53235792 | solution.py:183
  457.0 13.5 %collective-permute-done.1 = bf16[1,33,2048]{2,1,0:T(8,128)(2,1)S(1)} collective-permute-done((bf16[1,33,2048]{2,1,0:T(8,128)(2,1)S(1)}, bf16[1,33,2048]{2,1,0:T(8,128)(2,1)S(1)}, u32[]{:S(2)}, u32[]{:S(2)}) %collective-permute-start.1) | collective-permute-done | bytes 135200 | tf_op jit(solution)/shard_map/while/body/eval_jaxpr/ppermute | solution.py:12
  471.2 8.5 %conditional.13 = (bf16[1,33,2048]{2,1,0:T(8,128)(2,1)S(1)}, bf16[1,33,2048]{2,1,0:T(8,128)(2,1)S(1)}) conditional(s32[]{:T(128)} %convert_element_type.144, bf16[1,33,2048]{2,1,0:T(8,128)(2,1)S(1)} %get-tuple-element.973, (bf16[1,33,2048]{2,1,0:T(8,128)(2,1)S(1)}, s32[]{:T(128)}, bf16[6,1,33,2048]{3,2,1,0:T(8,128)(2,1)S(1)}, ...), branch_computations={%region_12.12_spmd, %region_13.14_spmd} | conditional | flops 554866688 | bytes 53235792 | solution.py:183
  483.6 13.5 %collective-permute-done.1 = bf16[1,33,2048]{2,1,0:T(8,128)(2,1)S(1)} collective-permute-done((bf16[1,33,2048]{2,1,0:T(8,128)(2,1)S(1)}, bf16[1,33,2048]{2,1,0:T(8,128)(2,1)S(1)}, u32[]{:S(2)}, u32[]{:S(2)}) %collective-permute-start.1) | collective-permute-done | bytes 135200 | tf_op jit(solution)/shard_map/while/body/eval_jaxpr/ppermute | solution.py:12
  497.8 8.5 %conditional.13 = (bf16[1,33,2048]{2,1,0:T(8,128)(2,1)S(1)}, bf16[1,33,2048]{2,1,0:T(8,128)(2,1)S(1)}) conditional(s32[]{:T(128)} %convert_element_type.144, bf16[1,33,2048]{2,1,0:T(8,128)(2,1)S(1)} %get-tuple-element.973, (bf16[1,33,2048]{2,1,0:T(8,128)(2,1)S(1)}, s32[]{:T(128)}, bf16[6,1,33,2048]{3,2,1,0:T(8,128)(2,1)S(1)}, ...), branch_computations={%region_12.12_spmd, %region_13.14_spmd} | conditional | flops 554866688 | bytes 53235792 | solution.py:183
  510.2 15.0 %collective-permute-done.1 = bf16[1,33,2048]{2,1,0:T(8,128)(2,1)S(1)} collective-permute-done((bf16[1,33,2048]{2,1,0:T(8,128)(2,1)S(1)}, bf16[1,33,2048]{2,1,0:T(8,128)(2,1)S(1)}, u32[]{:S(2)}, u32[]{:S(2)}) %collective-permute-start.1) | collective-permute-done | bytes 135200 | tf_op jit(solution)/shard_map/while/body/eval_jaxpr/ppermute | solution.py:12
  525.8 8.5 %conditional.13 = (bf16[1,33,2048]{2,1,0:T(8,128)(2,1)S(1)}, bf16[1,33,2048]{2,1,0:T(8,128)(2,1)S(1)}) conditional(s32[]{:T(128)} %convert_element_type.144, bf16[1,33,2048]{2,1,0:T(8,128)(2,1)S(1)} %get-tuple-element.973, (bf16[1,33,2048]{2,1,0:T(8,128)(2,1)S(1)}, s32[]{:T(128)}, bf16[6,1,33,2048]{3,2,1,0:T(8,128)(2,1)S(1)}, ...), branch_computations={%region_12.12_spmd, %region_13.14_spmd} | conditional | flops 554866688 | bytes 53235792 | solution.py:183
  541.5 6.8 %bitcast_convert_fusion = bf16[2048,2048]{1,0:T(8,128)(2,1)} fusion(bf16[6,1,33,2048]{3,2,1,0:T(8,128)(2,1)} %get-tuple-element.662, bf16[6,1,33,2048]{3,2,1,0:T(8,128)(2,1)S(1)} %get-tuple-element.1109), kind=kOutput, calls=%fused_computation.68 | convolution fusion | flops 1665138688 | bytes 10010624 | tf_op jit(solution)/shard_map/dot_general | solution.py:203
  560.0 6.8 %all-to-all-start = ((bf16[32,64,1024]{2,1,0:T(8,128)(2,1)}), bf16[32,64,1024]{2,1,0:T(8,128)(2,1)}, u32[]{:S(2)}, u32[]{:S(2)}) async-start(bf16[32,64,1024]{2,1,0:T(8,128)(2,1)} %bitcast.121), calls=%async_computation.1 | async-start | bytes 8388608 | tf_op jit(solution)/shard_map/all_to_all | solution.py:22
  567.5 69.4 %all-to-all-done = bf16[32,64,1024]{2,1,0:T(8,128)(2,1)} async-done(((bf16[32,64,1024]{2,1,0:T(8,128)(2,1)}), bf16[32,64,1024]{2,1,0:T(8,128)(2,1)}, u32[]{:S(2)}, u32[]{:S(2)}) %all-to-all-start) | async-done | bytes 4194336 | tf_op jit(solution)/shard_map/all_to_all | solution.py:22
  653.9 8.0 %all-to-all-done.1 = bf16[8,64,128]{2,1,0:T(8,128)(2,1)S(1)} async-done(((bf16[8,64,128]{2,1,0:T(8,128)(2,1)}), bf16[8,64,128]{2,1,0:T(8,128)(2,1)S(1)}, u32[]{:S(2)}, u32[]{:S(2)}) %all-to-all-start.1) | async-done | bytes 131104 | tf_op jit(solution)/shard_map/all_to_all | solution.py:22
  (401 shorter events, 420.0 us)
Async XLA Ops:
  7.2 82.0 %all-gather.3.cloned.1.call-start = ((), (), s32[]{:S(2)}) async-start(), calls=%async_computation.6 | async-start | bytes 8912896 | tf_op jit(solution)/shard_map/all_gather | solution.py:83
  7.9 654.5 %reduce-scatter.2.cloned.1.call-start = ((), (), s32[]{:S(2)}) async-start(), calls=%async_computation.5 | async-start | bytes 8650752 | tf_op jit(solution)/shard_map/reduce_scatter | solution.py:202
  101.3 4.9 collective-permute-start
  118.0 4.3 collective-permute-start
  134.2 4.1 collective-permute-start
  193.1 5.6 collective-permute-start
  205.5 4.1 collective-permute-start
  266.1 7.7 %collective-permute-start.1 = (bf16[1,33,2048]{2,1,0:T(8,128)(2,1)S(1)}, bf16[1,33,2048]{2,1,0:T(8,128)(2,1)S(1)}, u32[]{:S(2)}, u32[]{:S(2)}) collective-permute-start(bf16[1,33,2048]{2,1,0:T(8,128)(2,1)S(1)} %get-tuple-element.974), channel_id=1, source_target_pairs={{16,0},{32,16},{48,32},{64,48},{80,64},{96,80},{112,96},{17,1},{33... | collective-permute-start | bytes 405512 | tf_op jit(solution)/shard_map/while/body/eval_jaxpr/ppermute | solution.py:12
  274.4 7.2 %collective-permute-start.1 = (bf16[1,33,2048]{2,1,0:T(8,128)(2,1)S(1)}, bf16[1,33,2048]{2,1,0:T(8,128)(2,1)S(1)}, u32[]{:S(2)}, u32[]{:S(2)}) collective-permute-start(bf16[1,33,2048]{2,1,0:T(8,128)(2,1)S(1)} %get-tuple-element.974), channel_id=1, source_target_pairs={{16,0},{32,16},{48,32},{64,48},{80,64},{96,80},{112,96},{17,1},{33... | collective-permute-start | bytes 405512 | tf_op jit(solution)/shard_map/while/body/eval_jaxpr/ppermute | solution.py:12
  282.3 7.2 %collective-permute-start.1 = (bf16[1,33,2048]{2,1,0:T(8,128)(2,1)S(1)}, bf16[1,33,2048]{2,1,0:T(8,128)(2,1)S(1)}, u32[]{:S(2)}, u32[]{:S(2)}) collective-permute-start(bf16[1,33,2048]{2,1,0:T(8,128)(2,1)S(1)} %get-tuple-element.974), channel_id=1, source_target_pairs={{16,0},{32,16},{48,32},{64,48},{80,64},{96,80},{112,96},{17,1},{33... | collective-permute-start | bytes 405512 | tf_op jit(solution)/shard_map/while/body/eval_jaxpr/ppermute | solution.py:12
  290.2 8.2 %collective-permute-start.1 = (bf16[1,33,2048]{2,1,0:T(8,128)(2,1)S(1)}, bf16[1,33,2048]{2,1,0:T(8,128)(2,1)S(1)}, u32[]{:S(2)}, u32[]{:S(2)}) collective-permute-start(bf16[1,33,2048]{2,1,0:T(8,128)(2,1)S(1)} %get-tuple-element.974), channel_id=1, source_target_pairs={{16,0},{32,16},{48,32},{64,48},{80,64},{96,80},{112,96},{17,1},{33... | collective-permute-start | bytes 405512 | tf_op jit(solution)/shard_map/while/body/eval_jaxpr/ppermute | solution.py:12
  299.1 7.2 %collective-permute-start.1 = (bf16[1,33,2048]{2,1,0:T(8,128)(2,1)S(1)}, bf16[1,33,2048]{2,1,0:T(8,128)(2,1)S(1)}, u32[]{:S(2)}, u32[]{:S(2)}) collective-permute-start(bf16[1,33,2048]{2,1,0:T(8,128)(2,1)S(1)} %get-tuple-element.974), channel_id=1, source_target_pairs={{16,0},{32,16},{48,32},{64,48},{80,64},{96,80},{112,96},{17,1},{33... | collective-permute-start | bytes 405512 | tf_op jit(solution)/shard_map/while/body/eval_jaxpr/ppermute | solution.py:12
  307.0 7.2 %collective-permute-start.1 = (bf16[1,33,2048]{2,1,0:T(8,128)(2,1)S(1)}, bf16[1,33,2048]{2,1,0:T(8,128)(2,1)S(1)}, u32[]{:S(2)}, u32[]{:S(2)}) collective-permute-start(bf16[1,33,2048]{2,1,0:T(8,128)(2,1)S(1)} %get-tuple-element.974), channel_id=1, source_target_pairs={{16,0},{32,16},{48,32},{64,48},{80,64},{96,80},{112,96},{17,1},{33... | collective-permute-start | bytes 405512 | tf_op jit(solution)/shard_map/while/body/eval_jaxpr/ppermute | solution.py:12
  314.9 76.0 %collective-permute-start.1 = (bf16[1,33,2048]{2,1,0:T(8,128)(2,1)S(1)}, bf16[1,33,2048]{2,1,0:T(8,128)(2,1)S(1)}, u32[]{:S(2)}, u32[]{:S(2)}) collective-permute-start(bf16[1,33,2048]{2,1,0:T(8,128)(2,1)S(1)} %get-tuple-element.974), channel_id=1, source_target_pairs={{16,0},{32,16},{48,32},{64,48},{80,64},{96,80},{112,96},{17,1},{33... | collective-permute-start | bytes 405512 | tf_op jit(solution)/shard_map/while/body/eval_jaxpr/ppermute | solution.py:12
  400.0 17.4 %collective-permute-start.1 = (bf16[1,33,2048]{2,1,0:T(8,128)(2,1)S(1)}, bf16[1,33,2048]{2,1,0:T(8,128)(2,1)S(1)}, u32[]{:S(2)}, u32[]{:S(2)}) collective-permute-start(bf16[1,33,2048]{2,1,0:T(8,128)(2,1)S(1)} %get-tuple-element.974), channel_id=1, source_target_pairs={{16,0},{32,16},{48,32},{64,48},{80,64},{96,80},{112,96},{17,1},{33... | collective-permute-start | bytes 405512 | tf_op jit(solution)/shard_map/while/body/eval_jaxpr/ppermute | solution.py:12
  426.6 17.4 %collective-permute-start.1 = (bf16[1,33,2048]{2,1,0:T(8,128)(2,1)S(1)}, bf16[1,33,2048]{2,1,0:T(8,128)(2,1)S(1)}, u32[]{:S(2)}, u32[]{:S(2)}) collective-permute-start(bf16[1,33,2048]{2,1,0:T(8,128)(2,1)S(1)} %get-tuple-element.974), channel_id=1, source_target_pairs={{16,0},{32,16},{48,32},{64,48},{80,64},{96,80},{112,96},{17,1},{33... | collective-permute-start | bytes 405512 | tf_op jit(solution)/shard_map/while/body/eval_jaxpr/ppermute | solution.py:12
  453.2 17.4 %collective-permute-start.1 = (bf16[1,33,2048]{2,1,0:T(8,128)(2,1)S(1)}, bf16[1,33,2048]{2,1,0:T(8,128)(2,1)S(1)}, u32[]{:S(2)}, u32[]{:S(2)}) collective-permute-start(bf16[1,33,2048]{2,1,0:T(8,128)(2,1)S(1)} %get-tuple-element.974), channel_id=1, source_target_pairs={{16,0},{32,16},{48,32},{64,48},{80,64},{96,80},{112,96},{17,1},{33... | collective-permute-start | bytes 405512 | tf_op jit(solution)/shard_map/while/body/eval_jaxpr/ppermute | solution.py:12
  479.7 17.4 %collective-permute-start.1 = (bf16[1,33,2048]{2,1,0:T(8,128)(2,1)S(1)}, bf16[1,33,2048]{2,1,0:T(8,128)(2,1)S(1)}, u32[]{:S(2)}, u32[]{:S(2)}) collective-permute-start(bf16[1,33,2048]{2,1,0:T(8,128)(2,1)S(1)} %get-tuple-element.974), channel_id=1, source_target_pairs={{16,0},{32,16},{48,32},{64,48},{80,64},{96,80},{112,96},{17,1},{33... | collective-permute-start | bytes 405512 | tf_op jit(solution)/shard_map/while/body/eval_jaxpr/ppermute | solution.py:12
  506.3 18.9 %collective-permute-start.1 = (bf16[1,33,2048]{2,1,0:T(8,128)(2,1)S(1)}, bf16[1,33,2048]{2,1,0:T(8,128)(2,1)S(1)}, u32[]{:S(2)}, u32[]{:S(2)}) collective-permute-start(bf16[1,33,2048]{2,1,0:T(8,128)(2,1)S(1)} %get-tuple-element.974), channel_id=1, source_target_pairs={{16,0},{32,16},{48,32},{64,48},{80,64},{96,80},{112,96},{17,1},{33... | collective-permute-start | bytes 405512 | tf_op jit(solution)/shard_map/while/body/eval_jaxpr/ppermute | solution.py:12
  534.3 7.2 %collective-permute-start.1 = (bf16[1,33,2048]{2,1,0:T(8,128)(2,1)S(1)}, bf16[1,33,2048]{2,1,0:T(8,128)(2,1)S(1)}, u32[]{:S(2)}, u32[]{:S(2)}) collective-permute-start(bf16[1,33,2048]{2,1,0:T(8,128)(2,1)S(1)} %get-tuple-element.974), channel_id=1, source_target_pairs={{16,0},{32,16},{48,32},{64,48},{80,64},{96,80},{112,96},{17,1},{33... | collective-permute-start | bytes 405512 | tf_op jit(solution)/shard_map/while/body/eval_jaxpr/ppermute | solution.py:12
  549.0 11.1 %all-to-all-start.2 = ((f32[32,1,1]{2,1,0:T(1,128)}), f32[32,1,1]{2,1,0:T(1,128)S(1)}, u32[]{:S(2)}, u32[]{:S(2)}) async-start(f32[32,1,1]{2,1,0:T(1,128)} %broadcast_in_dim.76), calls=%async_computation.3 | async-start | bytes 32768 | tf_op jit(solution)/shard_map/all_to_all | solution.py:28
  560.0 76.8 %all-to-all-start = ((bf16[32,64,1024]{2,1,0:T(8,128)(2,1)}), bf16[32,64,1024]{2,1,0:T(8,128)(2,1)}, u32[]{:S(2)}, u32[]{:S(2)}) async-start(bf16[32,64,1024]{2,1,0:T(8,128)(2,1)} %bitcast.121), calls=%async_computation.1 | async-start | bytes 8388608 | tf_op jit(solution)/shard_map/all_to_all | solution.py:22
  638.1 10.9 %all-to-all-start.3 = ((bf16[8,1,1]{2,1,0:T(2,128)(2,1)}), bf16[8,1,1]{2,1,0:T(2,128)(2,1)S(1)}, u32[]{:S(2)}, u32[]{:S(2)}) async-start(bf16[8,1,1]{2,1,0:T(2,128)(2,1)} %transpose_reshape.3), calls=%async_computation.4 | async-start | bytes 8192 | tf_op jit(solution)/shard_map/all_to_all | solution.py:22
  649.0 12.8 %all-to-all-start.1 = ((bf16[8,64,128]{2,1,0:T(8,128)(2,1)}), bf16[8,64,128]{2,1,0:T(8,128)(2,1)S(1)}, u32[]{:S(2)}, u32[]{:S(2)}) async-start(bf16[8,64,128]{2,1,0:T(8,128)(2,1)} %copy.31), calls=%async_computation.2 | async-start | bytes 262144 | tf_op jit(solution)/shard_map/all_to_all | solution.py:22
  (14 other events, 67.5 us)
Sparse Core Ops, SparseCore 0:
  10.4 78.7 all-gather.2
  548.5 106.9 reduce-scatter.1
where the time goes:
time: 676 us; the launch traced here: 672 us
  waiting for transfers between devices  334 us (49%)
  matrix products  109 us (16%)
  local copies, waits for them, and re-layouts  67.7 us (10%)
  starting transfers between devices  54.7 us (8%)
  blocking collectives  36.6 us (5%)
  other arithmetic  27.2 us (4%)
  loops' own time  26.6 us (4%)
  between operations  15.9 us (2%)
    ppermute x26, waiting for transfers between devices, from_behind(): lax.ppermute(value, axis, [(source, source + steps) for source in range(i...  208 us
    all_to_all x3, waiting for transfers between devices, sent_and_summed(): lax.all_to_all(parts, axis, split_axis=0, concat_axis=0, tiled=True)  80.9 us
    all_gather x1, waiting for transfers between devices, local(): layer_full = lax.all_gather(layers[0], 'mp', axis=0, tiled=True)  42.4 us
    psum x1, blocking collectives, local(): lax.psum(jnp.sum(sample_total[sample_order].reshape(MB, per_batch), axis=...  36.6 us
    ppermute x26, starting transfers between devices, from_behind(): lax.ppermute(value, axis, [(source, source + steps) for source in range(i...  35.2 us
    dot_general x6, matrix products, backward_active(): jnp.dot(row_block.reshape(-1, model_width), layer_full, preferred_element...  30.4 us
    dot_general x6, matrix products, forward_layer(): jnp.dot(row_block.reshape(-1, model_width), weight, preferred_element_typ...  29.5 us
    dot_general x13, matrix products, lift_batch(): jnp.dot(rows_in.reshape(-1, in_width), encoder, preferred_element_type=jn...  26.7 us
  transfers between devices with their start and end apart: 32, of which 31 were waited for; matrix products, arithmetic and copies ran while one was open for 6% of the time, Pallas kernels for 0%

commit v1 on v0

--- a/solution.py
+++ b/solution.py
@@ -1,9 +1,17 @@
+import functools
 import jax
 import jax.numpy as jnp
 from jax import lax
 from jax.sharding import PartitionSpec as P
 
 MB = 6
+
+
+def measure_blocks(raw, row_axis):
+    return jax.lax.all_gather(raw, axis_name=row_axis).sum(axis=0)
+
+
+cut_the_outputs = functools.partial(measure_blocks, row_axis="mp")
 
 
 def from_behind(value, axis, steps):
@@ -86,8 +94,8 @@
         [jnp.ones((samp_dev, 1), jnp.float32), rank_mask.astype(jnp.float32)], axis=1
     )
     sample_total = jnp.sum(row_weight, axis=1)
-    batch_counts = lax.psum(
-        jnp.sum(sample_total[sample_order].reshape(MB, per_batch), axis=1), "mp"
+    batch_counts = cut_the_outputs(
+        jnp.sum(sample_total[sample_order].reshape(MB, per_batch), axis=1)
     )
 
     def picked_of(batch_slot):

time: 676 us -> 678 us (level)
    unnamed x0 -> x1, blocking collectives: none -> 36.7 us
    psum x1 -> x0, blocking collectives: 36.6 us -> none  [local(): lax.psum(jnp.sum(sample_total[sample_order].reshape(MB, per_batch), axis=...]
where the time goes in v1:
time: 678 us; the launch traced here: 674 us
  waiting for transfers between devices  334 us (49%)
  matrix products  109 us (16%)
  local copies, waits for them, and re-layouts  69.3 us (10%)
  starting transfers between devices  54.7 us (8%)
  blocking collectives  36.7 us (5%)
  other arithmetic  27.3 us (4%)
  loops' own time  26.5 us (4%)
  between operations  16.6 us (2%)
    ppermute x26, waiting for transfers between devices, from_behind(): lax.ppermute(value, axis, [(source, source + steps) for source in range(i...  209 us
    all_to_all x3, waiting for transfers between devices, sent_and_summed(): lax.all_to_all(parts, axis, split_axis=0, concat_axis=0, tiled=True)  80.9 us
    all_gather x1, waiting for transfers between devices, local(): layer_full = lax.all_gather(layers[0], 'mp', axis=0, tiled=True)  40 us
    unnamed x1, blocking collectives  36.7 us
    ppermute x26, starting transfers between devices, from_behind(): lax.ppermute(value, axis, [(source, source + steps) for source in range(i...  35.2 us
    dot_general x6, matrix products, backward_active(): jnp.dot(row_block.reshape(-1, model_width), layer_full, preferred_element...  30.4 us
    dot_general x6, matrix products, forward_layer(): jnp.dot(row_block.reshape(-1, model_width), weight, preferred_element_typ...  29.5 us
    dot_general x13, matrix products, lift_batch(): jnp.dot(rows_in.reshape(-1, in_width), encoder, preferred_element_type=jn...  26.7 us
  transfers between devices with their start and end apart: 32, of which 31 were waited for; matrix products, arithmetic and copies ran while one was open for 6% of the time, Pallas kernels for 0%

profile of v1, /device:TPU:4, one launch (start us, length us, event | category | flops | bytes accessed | tf_op | source)
XLA Modules:
  0.0 673.8 jit_solution(1165200505410530941)
XLA Ops:
  12.4 36.7 %all-reduce.1 = f32[96]{0:T(128)S(1)} all-reduce(f32[96]{0:T(128)S(1)} %dynamic-update-slice.5), channel_id=3, replica_groups=mesh['dp'=2,'section'=8,'mp'=16] {'mp'}, use_global_device_ids=true, to_apply=%add.1 | all-reduce | flops 96 | bytes 768
  49.2 40.0 %all-gather.4.cloned.1.call-done = bf16[1,2048,2048]{2,1,0:T(8,128)(2,1)} async-done(((bf16[1,128,2048]{2,1,0:T(8,128)(2,1)}), bf16[1,2048,2048]{2,1,0:T(8,128)(2,1)}) %all-gather.4.cloned.1.call-update) | async-done | bytes 8388624 | tf_op jit(solution)/shard_map/all_gather | solution.py:91
  89.4 174.6 %while.49 = (s32[]{:T(128)}, bf16[1,33,2048]{2,1,0:T(8,128)(2,1)S(1)}, bf16[6,1,33,2048]{3,2,1,0:T(8,128)(2,1)S(1)}, bf16[6,1,33,2048]{3,2,1,0:T(8,128)(2,1)S(1)...) while((s32[]{:T(128)}, ...), condition=%wide.region_5.0_spmd, body=%wide.region_0.5_spmd.sunk | while | flops 346843136 | bytes 14290341 | solution.py:138
  122.3 6.7 conditional.10
  220.4 6.7 conditional.10
  242.2 6.7 conditional.10
  253.1 6.7 conditional.10
  265.2 277.9 %while.50 = (s32[]{:T(128)}, bf16[1,33,2048]{2,1,0:T(8,128)(2,1)S(1)}, bf16[6,1,33,2048]{3,2,1,0:T(8,128)(2,1)}, bf16[6,1,33,1024]{3,2,1,0:T(8,128)(2,1)S(1)}, f...) while((s32[]{:T(128)}, ...), condition=%wide.region_15.16_spmd, body=%wide.region_8.15_spmd.sunk | while | flops 832231424 | bytes 80654912 | solution.py:204
  317.8 73.3 %collective-permute-done.1 = bf16[1,33,2048]{2,1,0:T(8,128)(2,1)S(1)} collective-permute-done((bf16[1,33,2048]{2,1,0:T(8,128)(2,1)S(1)}, bf16[1,33,2048]{2,1,0:T(8,128)(2,1)S(1)}, u32[]{:S(2)}, u32[]{:S(2)}) %collective-permute-start.1) | collective-permute-done | bytes 135200 | tf_op jit(solution)/shard_map/while/body/eval_jaxpr/ppermute | solution.py:20
  391.8 8.5 %conditional.13 = (bf16[1,33,2048]{2,1,0:T(8,128)(2,1)S(1)}, bf16[1,33,2048]{2,1,0:T(8,128)(2,1)S(1)}) conditional(s32[]{:T(128)} %convert_element_type.144, bf16[1,33,2048]{2,1,0:T(8,128)(2,1)S(1)} %get-tuple-element.973, (bf16[1,33,2048]{2,1,0:T(8,128)(2,1)S(1)}, s32[]{:T(128)}, bf16[6,1,33,2048]{3,2,1,0:T(8,128)(2,1)S(1)}, ...), branch_computations={%region_12.12_spmd, %region_13.14_spmd} | conditional | flops 554866688 | bytes 53235792 | solution.py:191
  404.2 13.8 %collective-permute-done.1 = bf16[1,33,2048]{2,1,0:T(8,128)(2,1)S(1)} collective-permute-done((bf16[1,33,2048]{2,1,0:T(8,128)(2,1)S(1)}, bf16[1,33,2048]{2,1,0:T(8,128)(2,1)S(1)}, u32[]{:S(2)}, u32[]{:S(2)}) %collective-permute-start.1) | collective-permute-done | bytes 135200 | tf_op jit(solution)/shard_map/while/body/eval_jaxpr/ppermute | solution.py:20
  418.6 8.5 %conditional.13 = (bf16[1,33,2048]{2,1,0:T(8,128)(2,1)S(1)}, bf16[1,33,2048]{2,1,0:T(8,128)(2,1)S(1)}) conditional(s32[]{:T(128)} %convert_element_type.144, bf16[1,33,2048]{2,1,0:T(8,128)(2,1)S(1)} %get-tuple-element.973, (bf16[1,33,2048]{2,1,0:T(8,128)(2,1)S(1)}, s32[]{:T(128)}, bf16[6,1,33,2048]{3,2,1,0:T(8,128)(2,1)S(1)}, ...), branch_computations={%region_12.12_spmd, %region_13.14_spmd} | conditional | flops 554866688 | bytes 53235792 | solution.py:191
  431.0 13.8 %collective-permute-done.1 = bf16[1,33,2048]{2,1,0:T(8,128)(2,1)S(1)} collective-permute-done((bf16[1,33,2048]{2,1,0:T(8,128)(2,1)S(1)}, bf16[1,33,2048]{2,1,0:T(8,128)(2,1)S(1)}, u32[]{:S(2)}, u32[]{:S(2)}) %collective-permute-start.1) | collective-permute-done | bytes 135200 | tf_op jit(solution)/shard_map/while/body/eval_jaxpr/ppermute | solution.py:20
  445.5 8.5 %conditional.13 = (bf16[1,33,2048]{2,1,0:T(8,128)(2,1)S(1)}, bf16[1,33,2048]{2,1,0:T(8,128)(2,1)S(1)}) conditional(s32[]{:T(128)} %convert_element_type.144, bf16[1,33,2048]{2,1,0:T(8,128)(2,1)S(1)} %get-tuple-element.973, (bf16[1,33,2048]{2,1,0:T(8,128)(2,1)S(1)}, s32[]{:T(128)}, bf16[6,1,33,2048]{3,2,1,0:T(8,128)(2,1)S(1)}, ...), branch_computations={%region_12.12_spmd, %region_13.14_spmd} | conditional | flops 554866688 | bytes 53235792 | solution.py:191
  457.8 13.8 %collective-permute-done.1 = bf16[1,33,2048]{2,1,0:T(8,128)(2,1)S(1)} collective-permute-done((bf16[1,33,2048]{2,1,0:T(8,128)(2,1)S(1)}, bf16[1,33,2048]{2,1,0:T(8,128)(2,1)S(1)}, u32[]{:S(2)}, u32[]{:S(2)}) %collective-permute-start.1) | collective-permute-done | bytes 135200 | tf_op jit(solution)/shard_map/while/body/eval_jaxpr/ppermute | solution.py:20
  472.3 8.5 %conditional.13 = (bf16[1,33,2048]{2,1,0:T(8,128)(2,1)S(1)}, bf16[1,33,2048]{2,1,0:T(8,128)(2,1)S(1)}) conditional(s32[]{:T(128)} %convert_element_type.144, bf16[1,33,2048]{2,1,0:T(8,128)(2,1)S(1)} %get-tuple-element.973, (bf16[1,33,2048]{2,1,0:T(8,128)(2,1)S(1)}, s32[]{:T(128)}, bf16[6,1,33,2048]{3,2,1,0:T(8,128)(2,1)S(1)}, ...), branch_computations={%region_12.12_spmd, %region_13.14_spmd} | conditional | flops 554866688 | bytes 53235792 | solution.py:191
  484.7 13.8 %collective-permute-done.1 = bf16[1,33,2048]{2,1,0:T(8,128)(2,1)S(1)} collective-permute-done((bf16[1,33,2048]{2,1,0:T(8,128)(2,1)S(1)}, bf16[1,33,2048]{2,1,0:T(8,128)(2,1)S(1)}, u32[]{:S(2)}, u32[]{:S(2)}) %collective-permute-start.1) | collective-permute-done | bytes 135200 | tf_op jit(solution)/shard_map/while/body/eval_jaxpr/ppermute | solution.py:20
  499.2 8.5 %conditional.13 = (bf16[1,33,2048]{2,1,0:T(8,128)(2,1)S(1)}, bf16[1,33,2048]{2,1,0:T(8,128)(2,1)S(1)}) conditional(s32[]{:T(128)} %convert_element_type.144, bf16[1,33,2048]{2,1,0:T(8,128)(2,1)S(1)} %get-tuple-element.973, (bf16[1,33,2048]{2,1,0:T(8,128)(2,1)S(1)}, s32[]{:T(128)}, bf16[6,1,33,2048]{3,2,1,0:T(8,128)(2,1)S(1)}, ...), branch_computations={%region_12.12_spmd, %region_13.14_spmd} | conditional | flops 554866688 | bytes 53235792 | solution.py:191
  511.5 15.3 %collective-permute-done.1 = bf16[1,33,2048]{2,1,0:T(8,128)(2,1)S(1)} collective-permute-done((bf16[1,33,2048]{2,1,0:T(8,128)(2,1)S(1)}, bf16[1,33,2048]{2,1,0:T(8,128)(2,1)S(1)}, u32[]{:S(2)}, u32[]{:S(2)}) %collective-permute-start.1) | collective-permute-done | bytes 135200 | tf_op jit(solution)/shard_map/while/body/eval_jaxpr/ppermute | solution.py:20
  527.5 8.5 %conditional.13 = (bf16[1,33,2048]{2,1,0:T(8,128)(2,1)S(1)}, bf16[1,33,2048]{2,1,0:T(8,128)(2,1)S(1)}) conditional(s32[]{:T(128)} %convert_element_type.144, bf16[1,33,2048]{2,1,0:T(8,128)(2,1)S(1)} %get-tuple-element.973, (bf16[1,33,2048]{2,1,0:T(8,128)(2,1)S(1)}, s32[]{:T(128)}, bf16[6,1,33,2048]{3,2,1,0:T(8,128)(2,1)S(1)}, ...), branch_computations={%region_12.12_spmd, %region_13.14_spmd} | conditional | flops 554866688 | bytes 53235792 | solution.py:191
  543.2 6.8 %bitcast_convert_fusion = bf16[2048,2048]{1,0:T(8,128)(2,1)} fusion(bf16[6,1,33,2048]{3,2,1,0:T(8,128)(2,1)} %get-tuple-element.662, bf16[6,1,33,2048]{3,2,1,0:T(8,128)(2,1)S(1)} %get-tuple-element.1109), kind=kOutput, calls=%fused_computation.68 | convolution fusion | flops 1665138688 | bytes 10010624 | tf_op jit(solution)/shard_map/dot_general | solution.py:211
  561.7 6.8 %all-to-all-start = ((bf16[32,64,1024]{2,1,0:T(8,128)(2,1)}), bf16[32,64,1024]{2,1,0:T(8,128)(2,1)}, u32[]{:S(2)}, u32[]{:S(2)}) async-start(bf16[32,64,1024]{2,1,0:T(8,128)(2,1)} %bitcast.122), calls=%async_computation.1 | async-start | bytes 8388608 | tf_op jit(solution)/shard_map/all_to_all | solution.py:30
  569.1 69.4 %all-to-all-done = bf16[32,64,1024]{2,1,0:T(8,128)(2,1)} async-done(((bf16[32,64,1024]{2,1,0:T(8,128)(2,1)}), bf16[32,64,1024]{2,1,0:T(8,128)(2,1)}, u32[]{:S(2)}, u32[]{:S(2)}) %all-to-all-start) | async-done | bytes 4194336 | tf_op jit(solution)/shard_map/all_to_all | solution.py:30
  655.5 8.0 %all-to-all-done.1 = bf16[8,64,128]{2,1,0:T(8,128)(2,1)S(1)} async-done(((bf16[8,64,128]{2,1,0:T(8,128)(2,1)}), bf16[8,64,128]{2,1,0:T(8,128)(2,1)S(1)}, u32[]{:S(2)}, u32[]{:S(2)}) %all-to-all-start.1) | async-done | bytes 131104 | tf_op jit(solution)/shard_map/all_to_all | solution.py:30
  (406 shorter events, 421.6 us)
Async XLA Ops:
  7.2 82.0 %all-gather.4.cloned.1.call-start = ((), (), s32[]{:S(2)}) async-start(), calls=%async_computation.6 | async-start | bytes 8912896 | tf_op jit(solution)/shard_map/all_gather | solution.py:91
  7.9 656.2 %reduce-scatter.2.cloned.1.call-start = ((), (), s32[]{:S(2)}) async-start(), calls=%async_computation.5 | async-start | bytes 8650752 | tf_op jit(solution)/shard_map/reduce_scatter | solution.py:210
  101.3 4.9 collective-permute-start
  118.0 4.3 collective-permute-start
  193.0 5.6 collective-permute-start
  205.4 4.1 collective-permute-start
  227.2 4.1 collective-permute-start
  266.0 7.7 %collective-permute-start.1 = (bf16[1,33,2048]{2,1,0:T(8,128)(2,1)S(1)}, bf16[1,33,2048]{2,1,0:T(8,128)(2,1)S(1)}, u32[]{:S(2)}, u32[]{:S(2)}) collective-permute-start(bf16[1,33,2048]{2,1,0:T(8,128)(2,1)S(1)} %get-tuple-element.974), channel_id=1, source_target_pairs={{16,0},{32,16},{48,32},{64,48},{80,64},{96,80},{112,96},{17,1},{33... | collective-permute-start | bytes 405512 | tf_op jit(solution)/shard_map/while/body/eval_jaxpr/ppermute | solution.py:20
  274.3 7.2 %collective-permute-start.1 = (bf16[1,33,2048]{2,1,0:T(8,128)(2,1)S(1)}, bf16[1,33,2048]{2,1,0:T(8,128)(2,1)S(1)}, u32[]{:S(2)}, u32[]{:S(2)}) collective-permute-start(bf16[1,33,2048]{2,1,0:T(8,128)(2,1)S(1)} %get-tuple-element.974), channel_id=1, source_target_pairs={{16,0},{32,16},{48,32},{64,48},{80,64},{96,80},{112,96},{17,1},{33... | collective-permute-start | bytes 405512 | tf_op jit(solution)/shard_map/while/body/eval_jaxpr/ppermute | solution.py:20
  282.2 7.2 %collective-permute-start.1 = (bf16[1,33,2048]{2,1,0:T(8,128)(2,1)S(1)}, bf16[1,33,2048]{2,1,0:T(8,128)(2,1)S(1)}, u32[]{:S(2)}, u32[]{:S(2)}) collective-permute-start(bf16[1,33,2048]{2,1,0:T(8,128)(2,1)S(1)} %get-tuple-element.974), channel_id=1, source_target_pairs={{16,0},{32,16},{48,32},{64,48},{80,64},{96,80},{112,96},{17,1},{33... | collective-permute-start | bytes 405512 | tf_op jit(solution)/shard_map/while/body/eval_jaxpr/ppermute | solution.py:20
  290.1 8.2 %collective-permute-start.1 = (bf16[1,33,2048]{2,1,0:T(8,128)(2,1)S(1)}, bf16[1,33,2048]{2,1,0:T(8,128)(2,1)S(1)}, u32[]{:S(2)}, u32[]{:S(2)}) collective-permute-start(bf16[1,33,2048]{2,1,0:T(8,128)(2,1)S(1)} %get-tuple-element.974), channel_id=1, source_target_pairs={{16,0},{32,16},{48,32},{64,48},{80,64},{96,80},{112,96},{17,1},{33... | collective-permute-start | bytes 405512 | tf_op jit(solution)/shard_map/while/body/eval_jaxpr/ppermute | solution.py:20
  299.0 7.2 %collective-permute-start.1 = (bf16[1,33,2048]{2,1,0:T(8,128)(2,1)S(1)}, bf16[1,33,2048]{2,1,0:T(8,128)(2,1)S(1)}, u32[]{:S(2)}, u32[]{:S(2)}) collective-permute-start(bf16[1,33,2048]{2,1,0:T(8,128)(2,1)S(1)} %get-tuple-element.974), channel_id=1, source_target_pairs={{16,0},{32,16},{48,32},{64,48},{80,64},{96,80},{112,96},{17,1},{33... | collective-permute-start | bytes 405512 | tf_op jit(solution)/shard_map/while/body/eval_jaxpr/ppermute | solution.py:20
  306.9 7.2 %collective-permute-start.1 = (bf16[1,33,2048]{2,1,0:T(8,128)(2,1)S(1)}, bf16[1,33,2048]{2,1,0:T(8,128)(2,1)S(1)}, u32[]{:S(2)}, u32[]{:S(2)}) collective-permute-start(bf16[1,33,2048]{2,1,0:T(8,128)(2,1)S(1)} %get-tuple-element.974), channel_id=1, source_target_pairs={{16,0},{32,16},{48,32},{64,48},{80,64},{96,80},{112,96},{17,1},{33... | collective-permute-start | bytes 405512 | tf_op jit(solution)/shard_map/while/body/eval_jaxpr/ppermute | solution.py:20
  314.8 76.3 %collective-permute-start.1 = (bf16[1,33,2048]{2,1,0:T(8,128)(2,1)S(1)}, bf16[1,33,2048]{2,1,0:T(8,128)(2,1)S(1)}, u32[]{:S(2)}, u32[]{:S(2)}) collective-permute-start(bf16[1,33,2048]{2,1,0:T(8,128)(2,1)S(1)} %get-tuple-element.974), channel_id=1, source_target_pairs={{16,0},{32,16},{48,32},{64,48},{80,64},{96,80},{112,96},{17,1},{33... | collective-permute-start | bytes 405512 | tf_op jit(solution)/shard_map/while/body/eval_jaxpr/ppermute | solution.py:20
  400.3 17.7 %collective-permute-start.1 = (bf16[1,33,2048]{2,1,0:T(8,128)(2,1)S(1)}, bf16[1,33,2048]{2,1,0:T(8,128)(2,1)S(1)}, u32[]{:S(2)}, u32[]{:S(2)}) collective-permute-start(bf16[1,33,2048]{2,1,0:T(8,128)(2,1)S(1)} %get-tuple-element.974), channel_id=1, source_target_pairs={{16,0},{32,16},{48,32},{64,48},{80,64},{96,80},{112,96},{17,1},{33... | collective-permute-start | bytes 405512 | tf_op jit(solution)/shard_map/while/body/eval_jaxpr/ppermute | solution.py:20
  427.1 17.7 %collective-permute-start.1 = (bf16[1,33,2048]{2,1,0:T(8,128)(2,1)S(1)}, bf16[1,33,2048]{2,1,0:T(8,128)(2,1)S(1)}, u32[]{:S(2)}, u32[]{:S(2)}) collective-permute-start(bf16[1,33,2048]{2,1,0:T(8,128)(2,1)S(1)} %get-tuple-element.974), channel_id=1, source_target_pairs={{16,0},{32,16},{48,32},{64,48},{80,64},{96,80},{112,96},{17,1},{33... | collective-permute-start | bytes 405512 | tf_op jit(solution)/shard_map/while/body/eval_jaxpr/ppermute | solution.py:20
  454.0 17.7 %collective-permute-start.1 = (bf16[1,33,2048]{2,1,0:T(8,128)(2,1)S(1)}, bf16[1,33,2048]{2,1,0:T(8,128)(2,1)S(1)}, u32[]{:S(2)}, u32[]{:S(2)}) collective-permute-start(bf16[1,33,2048]{2,1,0:T(8,128)(2,1)S(1)} %get-tuple-element.974), channel_id=1, source_target_pairs={{16,0},{32,16},{48,32},{64,48},{80,64},{96,80},{112,96},{17,1},{33... | collective-permute-start | bytes 405512 | tf_op jit(solution)/shard_map/while/body/eval_jaxpr/ppermute | solution.py:20
  480.8 17.7 %collective-permute-start.1 = (bf16[1,33,2048]{2,1,0:T(8,128)(2,1)S(1)}, bf16[1,33,2048]{2,1,0:T(8,128)(2,1)S(1)}, u32[]{:S(2)}, u32[]{:S(2)}) collective-permute-start(bf16[1,33,2048]{2,1,0:T(8,128)(2,1)S(1)} %get-tuple-element.974), channel_id=1, source_target_pairs={{16,0},{32,16},{48,32},{64,48},{80,64},{96,80},{112,96},{17,1},{33... | collective-permute-start | bytes 405512 | tf_op jit(solution)/shard_map/while/body/eval_jaxpr/ppermute | solution.py:20
  507.6 19.2 %collective-permute-start.1 = (bf16[1,33,2048]{2,1,0:T(8,128)(2,1)S(1)}, bf16[1,33,2048]{2,1,0:T(8,128)(2,1)S(1)}, u32[]{:S(2)}, u32[]{:S(2)}) collective-permute-start(bf16[1,33,2048]{2,1,0:T(8,128)(2,1)S(1)} %get-tuple-element.974), channel_id=1, source_target_pairs={{16,0},{32,16},{48,32},{64,48},{80,64},{96,80},{112,96},{17,1},{33... | collective-permute-start | bytes 405512 | tf_op jit(solution)/shard_map/while/body/eval_jaxpr/ppermute | solution.py:20
  536.0 7.2 %collective-permute-start.1 = (bf16[1,33,2048]{2,1,0:T(8,128)(2,1)S(1)}, bf16[1,33,2048]{2,1,0:T(8,128)(2,1)S(1)}, u32[]{:S(2)}, u32[]{:S(2)}) collective-permute-start(bf16[1,33,2048]{2,1,0:T(8,128)(2,1)S(1)} %get-tuple-element.974), channel_id=1, source_target_pairs={{16,0},{32,16},{48,32},{64,48},{80,64},{96,80},{112,96},{17,1},{33... | collective-permute-start | bytes 405512 | tf_op jit(solution)/shard_map/while/body/eval_jaxpr/ppermute | solution.py:20
  550.6 11.1 %all-to-all-start.2 = ((f32[32,1,1]{2,1,0:T(1,128)}), f32[32,1,1]{2,1,0:T(1,128)S(1)}, u32[]{:S(2)}, u32[]{:S(2)}) async-start(f32[32,1,1]{2,1,0:T(1,128)} %broadcast_in_dim.76), calls=%async_computation.3 | async-start | bytes 32768 | tf_op jit(solution)/shard_map/all_to_all | solution.py:36
  561.7 76.8 %all-to-all-start = ((bf16[32,64,1024]{2,1,0:T(8,128)(2,1)}), bf16[32,64,1024]{2,1,0:T(8,128)(2,1)}, u32[]{:S(2)}, u32[]{:S(2)}) async-start(bf16[32,64,1024]{2,1,0:T(8,128)(2,1)} %bitcast.122), calls=%async_computation.1 | async-start | bytes 8388608 | tf_op jit(solution)/shard_map/all_to_all | solution.py:30
  639.8 10.9 %all-to-all-start.3 = ((bf16[8,1,1]{2,1,0:T(2,128)(2,1)}), bf16[8,1,1]{2,1,0:T(2,128)(2,1)S(1)}, u32[]{:S(2)}, u32[]{:S(2)}) async-start(bf16[8,1,1]{2,1,0:T(2,128)(2,1)} %transpose_reshape.3), calls=%async_computation.4 | async-start | bytes 8192 | tf_op jit(solution)/shard_map/all_to_all | solution.py:30
  650.6 12.8 %all-to-all-start.1 = ((bf16[8,64,128]{2,1,0:T(8,128)(2,1)}), bf16[8,64,128]{2,1,0:T(8,128)(2,1)S(1)}, u32[]{:S(2)}, u32[]{:S(2)}) async-start(bf16[8,64,128]{2,1,0:T(8,128)(2,1)} %copy.31), calls=%async_computation.2 | async-start | bytes 262144 | tf_op jit(solution)/shard_map/all_to_all | solution.py:30
  (14 other events, 67.5 us)
Sparse Core Ops, SparseCore 0:
  10.4 78.7 all-gather.3
  550.1 106.8 reduce-scatter.1
